TPU v7x, 256 devices: a 4x2x16 block of a 4x16x16 slice. The times are simulated.
256 devices in a mesh: groups: 2 (over y), freq: 128 (over z, x, core).
Axes of the slice: x: 4, y: 2, z: 16, core: 2. Of those that a mesh axis runs over, the one named last changes fastest.
The devices are a block of a 4x16x16 slice.
Arguments:
- primary_one: bfloat16 [1024, 512, 512], P(('groups', 'freq')), parts along dimension 0, may hold values from -6 to 6
- primary_two: bfloat16 [1024, 512, 512], P(('groups', 'freq')), parts along dimension 0, may hold values from -6 to 6
- primary_three: bfloat16 [1024, 512, 512], P(('groups', 'freq')), parts along dimension 0, may hold values from -6 to 6
- window_start: int32 [3, 1024, 512], P(None, ('groups', 'freq')), parts along dimension 1, may hold values from 0 to 255
- window_end: int32 [3, 1024, 512], P(None, ('groups', 'freq')), parts along dimension 1, may hold values from 257 to 512
Outputs:
- predicted: bfloat16 [1024, 512, 512], P(('groups', 'freq')), parts along dimension 0
There are 2 independent parts, one for each index of `groups`. A program takes and returns all parts, laid end to end along the dimension named above; each array names one. Nothing has to cross between parts.
Inputs may be any that keep to these rules, and one draw needn't show every extreme that they name: window_start of a trace is below its window_end.
All inputs are finite; a program needn't handle non-finite values.
Results may differ from a plain program's by a relative error of at most 0.0089.
Values may be sent and summed in bfloat16 or wider, within the bound.
No kernel may reach another device: no remote copies, remote signals or barrier semaphores. Data moves between devices by JAX's collectives and lax.ppermute only.
A program may use at most 64 MiB of HBM per device.

v0:
```python
import jax
import jax.numpy as jnp
from jax import lax
from jax.sharding import PartitionSpec as P

F_DEV = 1


def sent_together(arrays, axis, split_dim, concat_dim, along):
    widths = [a.shape[along] for a in arrays]
    both = jnp.concatenate(arrays, axis=along)
    whole = lax.all_to_all(both, axis, split_axis=split_dim, concat_axis=concat_dim, tiled=True)
    return tuple(jnp.split(whole, [sum(widths[:k]) for k in range(1, len(widths))], axis=along))


def make_table(count, samples):
    waves = jnp.arange(1, count + 1, dtype=jnp.int32)[:, None]
    times = jnp.arange(samples, dtype=jnp.int32)[None, :]
    phase = waves * times % samples
    angle = 2.0 * jnp.pi / samples * phase.astype(jnp.float32)
    both = jnp.stack([jnp.cos(angle), -jnp.sin(angle)], axis=1)
    return both.reshape(2 * count, samples).astype(jnp.bfloat16)


def spectrum(traces, start, finish, table, count):
    sources, receivers, samples = traces.shape
    times = jnp.arange(samples, dtype=jnp.int32)
    inside = (times >= start[:, :, None]) & (times < finish[:, :, None])
    windowed = jnp.where(inside, traces, jnp.zeros_like(traces))
    flat = windowed.reshape(sources * receivers, samples)
    spec = lax.dot_general(
        table, flat, (((1,), (1,)), ((), ())), preferred_element_type=jnp.float32
    )
    spec = spec * (1.0 / jnp.sqrt(jnp.float32(samples)))
    return spec.astype(jnp.bfloat16).reshape(count, 2, sources, receivers)


def correlate(first, second):
    swapped = jnp.stack([first[:, 1], -first[:, 0]], axis=1)
    left = jnp.stack([first, swapped], axis=1)
    cross = jnp.einsum("fkcsr,fcur->fksu", left, second, preferred_element_type=jnp.float32)
    cross = cross * (1.0 / jnp.sqrt(jnp.float32(first.shape[3])))
    return cross.astype(jnp.bfloat16)


def convolve(cross, third):
    right = jnp.stack(
        [
            jnp.stack([third[:, 0], -third[:, 1]], axis=1),
            jnp.stack([third[:, 1], third[:, 0]], axis=1),
        ],
        axis=1,
    )
    multiple = jnp.einsum("fcsu,fkcur->fksr", cross, right, preferred_element_type=jnp.float32)
    multiple = multiple * (1.0 / jnp.sqrt(jnp.float32(third.shape[2])))
    return multiple.astype(jnp.bfloat16)


def on_device(primary_one, primary_two, primary_three, window_start, window_end):
    samples = primary_one.shape[2]
    count = F_DEV * lax.axis_size("freq")
    table = make_table(count, samples)
    spec_one = spectrum(primary_one, window_start[0], window_end[0], table, count)
    spec_two = spectrum(primary_two, window_start[1], window_end[1], table, count)
    spec_three = spectrum(primary_three, window_start[2], window_end[2], table, count)
    first, second = sent_together((spec_one, spec_two), "freq", 0, 2, 1)
    cross = correlate(first, second)
    third = lax.all_to_all(spec_three, "freq", split_axis=0, concat_axis=2, tiled=True)
    multiple = convolve(cross, third)
    piece = lax.all_to_all(multiple, "freq", split_axis=2, concat_axis=0, tiled=True)
    waves, parts, sources, receivers = piece.shape
    flat = piece.reshape(waves * parts, sources * receivers)
    timed = lax.dot_general(
        flat, table, (((0,), (0,)), ((), ())), preferred_element_type=jnp.float32
    )
    timed = timed * (1.0 / jnp.sqrt(jnp.float32(count)))
    return timed.astype(jnp.bfloat16).reshape(sources, receivers, samples)


def solution(mesh):
    return jax.shard_map(
        on_device,
        mesh=mesh,
        in_specs=(
            P(("groups", "freq"), None, None),
            P(("groups", "freq"), None, None),
            P(("groups", "freq"), None, None),
            P(None, ("groups", "freq"), None),
            P(None, ("groups", "freq"), None),
        ),
        out_specs=P(("groups", "freq"), None, None),
        check_vma=False,
    )
```

profile of v0, /device:TPU:33, one launch (start us, length us, event | category | flops | bytes accessed | tf_op | source)
XLA Modules:
  0.0 281.0 jit_solution(12625566358384556773)
XLA Ops:
  1.5 1.2 cosine_convert_fusion
  3.1 4.2 %fusion.1 = (bf16[4,512,512]{2,1,0:T(8,128)(2,1)S(1)}, bf16[4,512,512]{2,1,0:T(8,128)(2,1)S(1)}) fusion(bf16[4,512,512]{2,1,0:T(8,128)(2,1)} %param.7, s32[4,512]{1,0:T(4,128)S(1)} %get-tuple-element.17, s32[4,512]{1,0:T(4,128)S(1)} %get-tuple-element.14, bf16[4,512,512]{2,1,0:T(8,128)(2,1)} %param.5, s32[4,512]{1,0:T(4,128)S(1)} %get-tuple-element.16, ...), kind=kLoop, calls=%fused_computation.8 | loop fusion | flops 8388608 | bytes 8421376 | tf_op jit(solution)/shard_map/jit(_where)/select_n | solution.py:29
  7.3 1.7 fusion.6
  9.0 1.8 reshape.176
  10.9 1.8 copy.37
  12.7 31.0 %all-to-all-start = ((bf16[128,2,4,512]{3,1,2,0:T(2,128)(2,1)}), bf16[128,2,4,512]{3,1,2,0:T(2,128)(2,1)S(1)}, u32[]{:S(2)}, u32[]{:S(2)}) async-start(bf16[128,2,4,512]{3,1,2,0:T(2,128)(2,1)} %copy.37), calls=%async_computation | async-start | bytes 2097152 | tf_op jit(solution)/shard_map/all_to_all | solution.py:68
  43.7 1.7 fusion.7
  45.5 1.8 reshape.179
  50.1 1.7 fusion.8
  51.8 1.8 reshape.181
  54.5 3.2 %pad_maximum_fusion = bf16[128,4,4,512]{3,1,2,0:T(4,128)(2,1)} fusion(bf16[128,2,4,512]{3,1,2,0:T(2,128)(2,1)S(1)} %copy.41, bf16[128,2,4,512]{3,1,2,0:T(2,128)(2,1)S(1)} %copy.40), kind=kLoop, calls=%fused_computation.23 | loop fusion | flops 4194304 | bytes 4194304 | tf_op jit(solution)/shard_map/concatenate | solution.py:11
  57.8 36.9 %all-to-all-done = bf16[128,2,4,512]{3,1,2,0:T(2,128)(2,1)S(1)} async-done(((bf16[128,2,4,512]{3,1,2,0:T(2,128)(2,1)}), bf16[128,2,4,512]{3,1,2,0:T(2,128)(2,1)S(1)}, u32[]{:S(2)}, u32[]{:S(2)}) %all-to-all-start) | async-done | bytes 1048608 | tf_op jit(solution)/shard_map/all_to_all | solution.py:68
  94.7 11.8 %all-to-all-start.1 = ((bf16[128,4,4,512]{3,1,2,0:T(4,128)(2,1)}), bf16[128,4,4,512]{3,1,2,0:T(4,128)(2,1)S(1)}, u32[]{:S(2)}, u32[]{:S(2)}) async-start(bf16[128,4,4,512]{3,1,2,0:T(4,128)(2,1)} %pad_maximum_fusion), calls=%async_computation.1 | async-start | bytes 4194304 | tf_op jit(solution)/shard_map/all_to_all | solution.py:12
  106.5 2.5 fusion.30
  109.0 2.3 copy.51
  112.2 2.3 copy.50
  114.6 2.6 maximum_bitcast_fusion.12
  117.1 84.8 %all-to-all-done.1 = bf16[128,4,4,512]{3,1,2,0:T(4,128)(2,1)S(1)} async-done(((bf16[128,4,4,512]{3,1,2,0:T(4,128)(2,1)}), bf16[128,4,4,512]{3,1,2,0:T(4,128)(2,1)S(1)}, u32[]{:S(2)}, u32[]{:S(2)}) %all-to-all-start.1) | async-done | bytes 2097184 | tf_op jit(solution)/shard_map/all_to_all | solution.py:12
  202.0 1.5 fusion.29
  203.4 2.3 fusion.28
  207.9 4.9 %fusion.18 = bf16[1,2,512,512]{2,3,1,0:T(8,128)(2,1)} fusion(bf16[1,1,2,512,512]{3,4,2,1,0:T(8,128)(2,1)S(1)} %copy-done.2, bf16[1,1,2,512,512]{3,4,2,1,0:T(8,128)(2,1)S(1)} %copy-done.1, bf16[1,1,2,512,512]{4,3,2,1,0:T(8,128)(2,1)} %maximum_bitcast_fusion.14, bf16[1,1,2,512,512]{4,3,2,1,0:T(8,128)(2,1)S(1)} %bitcast.104, ...), kind=kOutput, calls=%fused_computation.33 | convolution fusion | flops 2151677952 | bytes 6291456 | tf_op jit(solution)/shard_map/fcsu,fkcur->fksr/dot_general | solution.py:54
  212.8 2.5 copy.46
  215.3 63.0 %all_to_all.51 = bf16[1,2,512,512]{3,1,0,2:T(2,128)(2,1)S(1)} all-to-all(bf16[1,2,512,512]{3,1,0,2:T(2,128)(2,1)S(1)} %copy.46), channel_id=1, replica_groups=mesh['groups'=2,'freq'=128] {'freq'}, dimensions={2} | all-to-all | bytes 2097152 | tf_op jit(solution)/shard_map/all_to_all | solution.py:70
  278.9 2.1 multiply_convert_fusion
  (22 shorter events, 9.2 us)
Async XLA Ops:
  12.7 82.0 %all-to-all-start = ((bf16[128,2,4,512]{3,1,2,0:T(2,128)(2,1)}), bf16[128,2,4,512]{3,1,2,0:T(2,128)(2,1)S(1)}, u32[]{:S(2)}, u32[]{:S(2)}) async-start(bf16[128,2,4,512]{3,1,2,0:T(2,128)(2,1)} %copy.37), calls=%async_computation | async-start | bytes 2097152 | tf_op jit(solution)/shard_map/all_to_all | solution.py:68
  47.3 1.6 copy-start
  94.7 107.3 %all-to-all-start.1 = ((bf16[128,4,4,512]{3,1,2,0:T(4,128)(2,1)}), bf16[128,4,4,512]{3,1,2,0:T(4,128)(2,1)S(1)}, u32[]{:S(2)}, u32[]{:S(2)}) async-start(bf16[128,4,4,512]{3,1,2,0:T(4,128)(2,1)} %pad_maximum_fusion), calls=%async_computation.1 | async-start | bytes 4194304 | tf_op jit(solution)/shard_map/all_to_all | solution.py:12
  205.9 1.3 copy-start.1
  206.0 1.9 copy-start.2
where the time goes:
time: 284 us; the launch traced here: 281 us
  waiting for transfers between devices  122 us (43%)
  blocking collectives  63 us (22%)
  starting transfers between devices  42.8 us (15%)
  local copies, waits for them, and re-layouts  26.7 us (9%)
  other arithmetic  14.4 us (5%)
  matrix products  12.1 us (4%)
    all_to_all x1, waiting for transfers between devices, sent_together(): lax.all_to_all(both, axis, split_axis=split_dim, concat_axis=concat_dim,...  84.8 us
    all_to_all x1, blocking collectives, on_device(): lax.all_to_all(multiple, 'freq', split_axis=2, concat_axis=0, tiled=True)  63 us
    all_to_all x1, waiting for transfers between devices, on_device(): lax.all_to_all(spec_three, 'freq', split_axis=0, concat_axis=2, tiled=True)  36.9 us
    all_to_all x1, starting transfers between devices, on_device(): lax.all_to_all(spec_three, 'freq', split_axis=0, concat_axis=2, tiled=True)  31 us
    all_to_all x1, starting transfers between devices, sent_together(): lax.all_to_all(both, axis, split_axis=split_dim, concat_axis=concat_dim,...  11.8 us
    reshape x6, local copies, waits for them, and re-layouts, spectrum(): return spec.astype(jnp.bfloat16).reshape(count, 2, sources, receivers)  9.02 us
    unnamed x11, local copies, waits for them, and re-layouts  6.66 us
  transfers between devices with their start and end apart: 2, of which 2 were waited for; matrix products, arithmetic and copies ran while one was open for 8% of the time, Pallas kernels for 0%

commit v1 on v0

v1 whole, which is shorter than its diff:
```python
import jax
import jax.numpy as jnp
import numpy as np
from jax import lax
from jax.experimental import pallas as pl
from jax.experimental.pallas import tpu as pltpu
from jax.sharding import PartitionSpec as P

BF = jnp.bfloat16
F32 = jnp.float32
LANE = 128
VMEM_LIMIT = 56 * 1024 * 1024


def make_table(count, samples):
    waves = np.arange(1, count + 1, dtype=np.int64)[:, None]
    times = np.arange(samples, dtype=np.int64)[None, :]
    angle = 2.0 * np.pi / samples * (waves * times % samples)
    both = np.stack([np.cos(angle), -np.sin(angle)], axis=1)
    return both.reshape(2 * count, samples).astype(np.float32)


def swap_matrix(size, half):
    out = np.zeros((size, size), np.float32)
    for base in range(0, size, 2 * half):
        for k in range(half):
            out[base + k, base + half + k] = -1.0
            out[base + half + k, base + k] = 1.0
    return out


def spectra(primaries, window_start, window_end, table):
    sets = len(primaries)
    sources, receivers, samples = primaries[0].shape
    waves = table.shape[0]
    rows = waves * sources
    lanes = receivers // LANE
    scale = 1.0 / float(np.sqrt(samples))

    def body(*refs):
        traces = refs[:sets]
        start_ref, end_ref, table_ref, out_ref, col_ref, acc_ref = refs[sets:]
        step = pl.program_id(0)

        @pl.when(step == 0)
        def _():
            for s in range(sources):
                lines = []
                for j in range(sets):
                    lines.append(start_ref[j, s : s + 1, :])
                    lines.append(end_ref[j, s : s + 1, :])
                lines.append(jnp.zeros((8 - 2 * sets, receivers), jnp.int32))
                col_ref[s] = jnp.transpose(jnp.concatenate(lines, axis=0))

        times = lax.broadcasted_iota(jnp.int32, (receivers, samples), 1)
        cols = col_ref[step]
        for j in range(sets):
            start = cols[:, 2 * j : 2 * j + 1]
            finish = cols[:, 2 * j + 1 : 2 * j + 2]
            inside = (times >= start) & (times < finish)
            x = traces[j][0].astype(F32)
            x = jnp.where(inside, x, 0.0).astype(BF)
            spec = lax.dot_general(
                table_ref[...], x, (((1,), (1,)), ((), ())), preferred_element_type=F32
            )
            spec = spec * scale
            for b in range(lanes):
                acc_ref[j * lanes + b, pl.ds(step, waves, stride=sources), :] = spec[:, b * LANE : (b + 1) * LANE]

        @pl.when(step == sources - 1)
        def _():
            for k in range(sets * lanes):
                out_ref[:, k * LANE : (k + 1) * LANE] = acc_ref[k].astype(BF)

    return pl.pallas_call(
        body,
        grid=(sources,),
        in_specs=[pl.BlockSpec((1, receivers, samples), lambda i: (i, 0, 0))] * sets
        + [
            pl.BlockSpec(window_start.shape, lambda i: (0, 0, 0)),
            pl.BlockSpec(window_end.shape, lambda i: (0, 0, 0)),
            pl.BlockSpec(table.shape, lambda i: (0, 0)),
        ],
        out_specs=pl.BlockSpec((rows, sets * receivers), lambda i: (0, 0)),
        out_shape=jax.ShapeDtypeStruct((rows, sets * receivers), BF),
        scratch_shapes=[
            pltpu.VMEM((sources, receivers, 8), jnp.int32),
            pltpu.VMEM((sets * lanes, rows, LANE), F32),
        ],
        compiler_params=pltpu.CompilerParams(vmem_limit_bytes=VMEM_LIMIT),
        name="spectra",
    )(*primaries, window_start, window_end, table)


def product(received, swap, receivers, sources):
    rows = received.shape[0]
    block = swap.shape[0]
    in_scale = 1.0 / float(np.sqrt(receivers))
    out_scale = 1.0 / float(np.sqrt(sources))

    def turned(x, swap_ref):
        parts = [
            jnp.dot(swap_ref[...], x[k : k + block], preferred_element_type=F32).astype(BF)
            for k in range(0, rows, block)
        ]
        return jnp.concatenate(parts, axis=0)

    def body(x_ref, swap_ref, out_ref, q_re, q_im):
        second = x_ref[:, receivers : 2 * receivers]
        third = x_ref[:, 2 * receivers : 3 * receivers]
        over_rows = (((0,), (0,)), ((), ()))
        re = lax.dot_general(second, third, over_rows, preferred_element_type=F32)
        q_re[...] = (re * in_scale).astype(BF)
        im = lax.dot_general(second, turned(third, swap_ref), over_rows, preferred_element_type=F32)
        q_im[...] = (im * -in_scale).astype(BF)
        first = x_ref[:, :receivers]
        total = jnp.dot(first, q_re[...], preferred_element_type=F32)
        total = total + jnp.dot(turned(first, swap_ref), q_im[...], preferred_element_type=F32)
        out_ref[...] = (total * out_scale).astype(BF)

    return pl.pallas_call(
        body,
        out_shape=jax.ShapeDtypeStruct((rows, receivers), BF),
        scratch_shapes=[pltpu.VMEM((receivers, receivers), BF)] * 2,
        compiler_params=pltpu.CompilerParams(vmem_limit_bytes=VMEM_LIMIT),
        name="product",
    )(received, swap)


def inverse(returned, table, sources):
    rows, receivers = returned.shape
    waves, samples = table.shape
    lanes = receivers // LANE
    scale = 1.0 / float(np.sqrt(waves // 2))

    def body(x_ref, table_ref, out_ref, wide_ref):
        step = pl.program_id(0)

        @pl.when(step == 0)
        def _():
            for b in range(lanes):
                wide_ref[b] = x_ref[:, b * LANE : (b + 1) * LANE].astype(F32)

        parts = [wide_ref[b, pl.ds(step, waves, stride=sources), :].astype(BF) for b in range(lanes)]
        x = jnp.concatenate(parts, axis=1)
        timed = lax.dot_general(x, table_ref[...], (((0,), (0,)), ((), ())), preferred_element_type=F32)
        out_ref[0] = (timed * scale).astype(BF)

    return pl.pallas_call(
        body,
        grid=(sources,),
        in_specs=[
            pl.BlockSpec((rows, receivers), lambda i: (0, 0)),
            pl.BlockSpec((waves, samples), lambda i: (0, 0)),
        ],
        out_specs=pl.BlockSpec((1, receivers, samples), lambda i: (i, 0, 0)),
        out_shape=jax.ShapeDtypeStruct((sources, receivers, samples), BF),
        scratch_shapes=[pltpu.VMEM((lanes, rows, LANE), F32)],
        compiler_params=pltpu.CompilerParams(vmem_limit_bytes=VMEM_LIMIT),
        name="inverse",
    )(returned, table)


def on_device(primary_one, primary_two, primary_three, window_start, window_end):
    sources, receivers, samples = primary_one.shape
    count = lax.axis_size("freq")
    table = jnp.asarray(make_table(count, samples), BF)
    swap = jnp.asarray(swap_matrix(256, sources), BF)
    sent = spectra((primary_one, primary_two, primary_three), window_start, window_end, table)
    received = lax.all_to_all(sent, "freq", split_axis=0, concat_axis=0, tiled=True)
    multiple = product(received, swap, receivers, sources * count)
    returned = lax.all_to_all(multiple, "freq", split_axis=0, concat_axis=0, tiled=True)
    return inverse(returned, table, sources)


def solution(mesh):
    split = P(("groups", "freq"), None, None)
    windows = P(None, ("groups", "freq"), None)
    return jax.shard_map(
        on_device,
        mesh=mesh,
        in_specs=(split, split, split, windows, windows),
        out_specs=split,
        check_vma=False,
    )
```

time: 284 us -> 256 us (0.901)
  blocking collectives: 63 us -> 235 us
  waiting for transfers between devices: 122 us -> 0 us
  starting transfers between devices: 42.8 us -> 0 us
  local copies, waits for them, and re-layouts: 26.7 us -> 0 us
  Pallas kernels: 0 us -> 18.6 us
  other arithmetic: 14.4 us -> 0 us
  matrix products: 12.1 us -> 0 us
    all_to_all x1 -> x2, blocking collectives: 63 us -> 235 us  [the longest x1 171 us: on_device(): lax.all_to_all(sent, 'freq', split_axis=0, concat_axis=0, tiled=True)]
    all_to_all x2 -> x0, waiting for transfers between devices: 122 us -> none  [the longest x1 84.8 us: sent_together(): lax.all_to_all(both, axis, split_axis=split_dim, concat_axis=concat_dim,...]
    all_to_all x2 -> x0, starting transfers between devices: 42.8 us -> none  [the longest x1 31 us: on_device(): lax.all_to_all(spec_three, 'freq', split_axis=0, concat_axis=2, tiled=True)]
    pallas_call x0 -> x3, Pallas kernels: none -> 18.6 us  [the longest x1 8.82 us: spectra(): pl.pallas_call(body, grid=(sources,), in_specs=[pl.BlockSpec((1, receiver...]
    dot_general x5 -> x0, matrix products: 12.1 us -> none  [the longest x3 5.15 us: spectrum(): lax.dot_general(table, flat, (((1,), (1,)), ((), ())), preferred_element_...]
    reshape x6 -> x0, local copies, waits for them, and re-layouts: 9.02 us -> none  [spectrum(): return spec.astype(jnp.bfloat16).reshape(count, 2, sources, receivers)]
    unnamed x11 -> x0, local copies, waits for them, and re-layouts: 6.66 us -> none
    select_n x2 -> x0, other arithmetic: 5.4 us -> none  [spectrum(): windowed = jnp.where(inside, traces, jnp.zeros_like(traces))]
  transfers between devices with their start and end apart: 2 -> 0, of which waited for: 2 -> 0; matrix products, arithmetic and copies ran while one was open for 8% -> 0% of each run, Pallas kernels for 0% -> 0%
where the time goes in v1:
time: 256 us; the launch traced here: 254 us
  blocking collectives  235 us (92%)
  Pallas kernels  18.6 us (7%)
    all_to_all x1, blocking collectives, on_device(): lax.all_to_all(sent, 'freq', split_axis=0, concat_axis=0, tiled=True)  171 us
    all_to_all x1, blocking collectives, on_device(): lax.all_to_all(multiple, 'freq', split_axis=0, concat_axis=0, tiled=True)  64 us
    pallas_call x1, Pallas kernels, spectra(): pl.pallas_call(body, grid=(sources,), in_specs=[pl.BlockSpec((1, receiver...  8.82 us
    pallas_call x1, Pallas kernels, product(): pl.pallas_call(body, out_shape=jax.ShapeDtypeStruct((rows, receivers), BF...  5.77 us

profile of v1, /device:TPU:33, one launch (start us, length us, event | category | flops | bytes accessed | tf_op | source)
XLA Modules:
  0.0 253.5 jit_solution(10802920625741370951)
XLA Ops:
  0.0 8.8 %spectra.1 = bf16[1024,1536]{1,0:T(8,128)(2,1)} custom-call(bf16[4,512,512]{2,1,0:T(8,128)(2,1)} %refs_0_.1, bf16[4,512,512]{2,1,0:T(8,128)(2,1)} %refs_1_.1, bf16[4,512,512]{2,1,0:T(8,128)(2,1)} %refs_2_.1, s32[3,4,512]{2,1,0:T(4,128)} %refs_3_.1, s32[3,4,512]{2,1,0:T(4,128)} %refs_4_.1, bf16[256,512]{1,0:T(8,128)(2,1)} %constant.4.clone.refs_5_.table_ref), custom_call_target="tpu_custom_call" | custom-call | tf_op jit(solution)/shard_map/spectra/pallas_call | solution.py:75
  8.8 170.9 %all_to_all.22 = bf16[128,8,1536]{2,1,0:T(8,128)(2,1)} all-to-all(bf16[128,8,1536]{2,1,0:T(8,128)(2,1)} %bitcast.5), channel_id=1, replica_groups=mesh['groups'=2,'freq'=128] {'freq'}, dimensions={0} | all-to-all | bytes 6291456 | tf_op jit(solution)/shard_map/all_to_all | solution.py:170
  179.7 5.8 %product.1 = bf16[1024,512]{1,0:T(8,128)(2,1)} custom-call(bf16[1024,1536]{1,0:T(8,128)(2,1)} %bitcast.4, bf16[256,256]{1,0:T(8,128)(2,1)} %constant.5.clone.swap_ref), custom_call_target="tpu_custom_call" | custom-call | tf_op jit(solution)/shard_map/product/pallas_call | solution.py:121
  185.5 64.0 %all_to_all.23 = bf16[128,8,512]{2,1,0:T(8,128)(2,1)} all-to-all(bf16[128,8,512]{2,1,0:T(8,128)(2,1)} %bitcast.7), channel_id=1, replica_groups=mesh['groups'=2,'freq'=128] {'freq'}, dimensions={0} | all-to-all | bytes 2097152 | tf_op jit(solution)/shard_map/all_to_all | solution.py:172
  249.5 4.0 %inverse.1 = bf16[4,512,512]{2,1,0:T(8,128)(2,1)} custom-call(bf16[1024,512]{1,0:T(8,128)(2,1)} %bitcast.6, bf16[256,512]{1,0:T(8,128)(2,1)} %constant.4.clone.refs_5_.table_ref), custom_call_target="tpu_custom_call" | custom-call | tf_op jit(solution)/shard_map/inverse/pallas_call | solution.py:149

commit v2 on v1

v2 whole, which is shorter than its diff:
```python
import jax
import jax.numpy as jnp
import numpy as np
from jax import lax
from jax.experimental import pallas as pl
from jax.experimental.pallas import tpu as pltpu
from jax.sharding import PartitionSpec as P

BF = jnp.bfloat16
F32 = jnp.float32
LANE = 128
VMEM_LIMIT = 56 * 1024 * 1024


def make_table(count, samples):
    waves = np.arange(1, count + 1, dtype=np.int64)[:, None]
    times = np.arange(samples, dtype=np.int64)[None, :]
    angle = 2.0 * np.pi / samples * (waves * times % samples)
    both = np.stack([np.cos(angle), -np.sin(angle)], axis=1)
    return both.reshape(2 * count, samples).astype(np.float32)


def swap_matrix(size, half):
    out = np.zeros((size, size), np.float32)
    for base in range(0, size, 2 * half):
        for k in range(half):
            out[base + k, base + half + k] = -1.0
            out[base + half + k, base + k] = 1.0
    return out


def spectra(primaries, window_start, window_end, table):
    sets = len(primaries)
    sources, receivers, samples = primaries[0].shape
    waves = table.shape[0]
    rows = waves * sources
    lanes = receivers // LANE
    half = samples // 2
    scale = 1.0 / float(np.sqrt(samples))

    def body(*refs):
        traces = refs[:sets]
        start_ref, end_ref, table_ref, out_ref, buf_ref, col_ref, acc_ref, sems = refs[sets:]

        def fetch(j, s):
            return pltpu.make_async_copy(traces[j].at[s], buf_ref.at[j, s], sems.at[j, s])

        for j in range(sets):
            for s in range(sources):
                fetch(j, s).start()
        for s in range(sources):
            lines = []
            for j in range(sets):
                lines.append(start_ref[j, s : s + 1, :])
                lines.append(end_ref[j, s : s + 1, :] - half)
            lines.append(jnp.zeros((8 - 2 * sets, receivers), jnp.int32))
            col_ref[s] = jnp.transpose(jnp.concatenate(lines, axis=0).astype(F32))

        times = lax.broadcasted_iota(jnp.int32, (receivers, half), 1).astype(F32).astype(BF)
        zero = jnp.zeros((receivers, half), BF)

        def one(s, j):
            fetch(j, s).wait()
            cols = col_ref[s]
            start = jnp.broadcast_to(cols[:, 2 * j : 2 * j + 1], (receivers, half)).astype(BF)
            finish = jnp.broadcast_to(cols[:, 2 * j + 1 : 2 * j + 2], (receivers, half)).astype(BF)
            early = jnp.where(times >= start, buf_ref[j, s, :, :half], zero)
            late = jnp.where(times < finish, buf_ref[j, s, :, half:], zero)
            across = (((1,), (1,)), ((), ()))
            kept = jnp.concatenate([early, late], axis=1)
            spec = lax.dot_general(table_ref[...], kept, across, preferred_element_type=F32)
            for b in range(lanes):
                acc_ref[b, pl.ds(s, waves, stride=sources), :] = spec[:, b * LANE : (b + 1) * LANE] * scale

        for j in range(sets):
            @pl.loop(0, sources)
            def _(s):
                one(s, j)
            for b in range(lanes):
                at = j * receivers + b * LANE
                out_ref[:, at : at + LANE] = acc_ref[b].astype(BF)

    vmem = pl.BlockSpec(memory_space=pltpu.VMEM)
    return pl.pallas_call(
        body,
        in_specs=[pl.BlockSpec(memory_space=pl.ANY)] * sets + [vmem] * 3,
        out_specs=vmem,
        out_shape=pltpu.VMEM((rows, sets * receivers), BF),
        scratch_shapes=[
            pltpu.VMEM((sets, sources, receivers, samples), BF),
            pltpu.VMEM((sources, receivers, 8), F32),
            pltpu.VMEM((lanes, rows, LANE), F32),
            pltpu.SemaphoreType.DMA((sets, sources)),
        ],
        compiler_params=pltpu.CompilerParams(vmem_limit_bytes=VMEM_LIMIT),
        name="spectra",
    )(*primaries, window_start, window_end, table)


def product(received, swap, receivers, sources):
    rows = received.shape[0]
    block = swap.shape[0]
    in_scale = 1.0 / float(np.sqrt(receivers))
    out_scale = 1.0 / float(np.sqrt(sources))

    def turned(x, swap_ref):
        parts = [
            jnp.dot(swap_ref[...], x[k : k + block], preferred_element_type=F32).astype(BF)
            for k in range(0, rows, block)
        ]
        return jnp.concatenate(parts, axis=0)

    def body(x_ref, swap_ref, out_ref, q_re, q_im):
        second = x_ref[:, receivers : 2 * receivers]
        third = x_ref[:, 2 * receivers : 3 * receivers]
        over_rows = (((0,), (0,)), ((), ()))
        re = lax.dot_general(second, third, over_rows, preferred_element_type=F32)
        q_re[...] = (re * in_scale).astype(BF)
        im = lax.dot_general(second, turned(third, swap_ref), over_rows, preferred_element_type=F32)
        q_im[...] = (im * -in_scale).astype(BF)
        first = x_ref[:, :receivers]
        total = jnp.dot(first, q_re[...], preferred_element_type=F32)
        total = total + jnp.dot(turned(first, swap_ref), q_im[...], preferred_element_type=F32)
        out_ref[...] = (total * out_scale).astype(BF)

    vmem = pl.BlockSpec(memory_space=pltpu.VMEM)
    return pl.pallas_call(
        body,
        in_specs=[vmem, vmem],
        out_specs=vmem,
        out_shape=pltpu.VMEM((rows, receivers), BF),
        scratch_shapes=[pltpu.VMEM((receivers, receivers), BF)] * 2,
        compiler_params=pltpu.CompilerParams(vmem_limit_bytes=VMEM_LIMIT),
        name="product",
    )(received, swap)


def inverse(returned, table, sources):
    rows, receivers = returned.shape
    waves, samples = table.shape
    lanes = receivers // LANE
    scale = 1.0 / float(np.sqrt(waves // 2))

    def body(x_ref, table_ref, out_ref, wide_ref, timed_ref, sems):
        for b in range(lanes):
            wide_ref[b] = x_ref[:, b * LANE : (b + 1) * LANE].astype(F32)
        copies = []
        for s in range(sources):
            parts = [wide_ref[b, pl.ds(s, waves, stride=sources), :].astype(BF) for b in range(lanes)]
            x = jnp.concatenate(parts, axis=1)
            timed = lax.dot_general(x, table_ref[...], (((0,), (0,)), ((), ())), preferred_element_type=F32)
            timed_ref[s] = (timed * scale).astype(BF)
            copy = pltpu.make_async_copy(timed_ref.at[s], out_ref.at[s], sems.at[s])
            copy.start()
            copies.append(copy)
        for copy in copies:
            copy.wait()

    vmem = pl.BlockSpec(memory_space=pltpu.VMEM)
    return pl.pallas_call(
        body,
        in_specs=[vmem, vmem],
        out_specs=pl.BlockSpec(memory_space=pl.ANY),
        out_shape=jax.ShapeDtypeStruct((sources, receivers, samples), BF),
        scratch_shapes=[
            pltpu.VMEM((lanes, rows, LANE), F32),
            pltpu.VMEM((sources, receivers, samples), BF),
            pltpu.SemaphoreType.DMA((sources,)),
        ],
        compiler_params=pltpu.CompilerParams(vmem_limit_bytes=VMEM_LIMIT),
        name="inverse",
    )(returned, table)


def on_device(primary_one, primary_two, primary_three, window_start, window_end):
    sources, receivers, samples = primary_one.shape
    count = lax.axis_size("freq")
    table = jnp.asarray(make_table(count, samples), BF)
    swap = jnp.asarray(swap_matrix(256, sources), BF)
    sent = spectra((primary_one, primary_two, primary_three), window_start, window_end, table)
    received = lax.all_to_all(sent, "freq", split_axis=0, concat_axis=0, tiled=True)
    received = pltpu.with_memory_space_constraint(received, pltpu.VMEM)
    multiple = product(received, swap, receivers, sources * count)
    returned = lax.all_to_all(multiple, "freq", split_axis=0, concat_axis=0, tiled=True)
    returned = pltpu.with_memory_space_constraint(returned, pltpu.VMEM)
    return inverse(returned, table, sources)


def solution(mesh):
    split = P(("groups", "freq"), None, None)
    windows = P(None, ("groups", "freq"), None)
    return jax.shard_map(
        on_device,
        mesh=mesh,
        in_specs=(split, split, split, windows, windows),
        out_specs=split,
        check_vma=False,
    )
```

time: 256 us -> 251 us (0.980)
  Pallas kernels: 18.6 us -> 14.2 us
    pallas_call x3, Pallas kernels: 18.6 us -> 14.2 us  [the longest x1 7.66 us: spectra(): pl.pallas_call(body, in_specs=[pl.BlockSpec(memory_space=pl.ANY)] * sets...]
where the time goes in v2:
time: 251 us; the launch traced here: 249 us
  blocking collectives  234 us (93%)
  Pallas kernels  14.2 us (6%)
    all_to_all x1, blocking collectives, on_device(): lax.all_to_all(sent, 'freq', split_axis=0, concat_axis=0, tiled=True)  171 us
    all_to_all x1, blocking collectives, on_device(): lax.all_to_all(multiple, 'freq', split_axis=0, concat_axis=0, tiled=True)  63.7 us
    pallas_call x1, Pallas kernels, spectra(): pl.pallas_call(body, in_specs=[pl.BlockSpec(memory_space=pl.ANY)] * sets...  7.66 us

profile of v2, /device:TPU:33, one launch (start us, length us, event | category | flops | bytes accessed | tf_op | source)
XLA Modules:
  0.0 248.5 jit_solution(5339421728582100884)
XLA Ops:
  0.0 7.7 %spectra.1 = bf16[1024,1536]{1,0:T(8,128)(2,1)S(1)} custom-call(bf16[4,512,512]{2,1,0:T(8,128)(2,1)} %refs_0_.1, bf16[4,512,512]{2,1,0:T(8,128)(2,1)} %refs_1_.1, bf16[4,512,512]{2,1,0:T(8,128)(2,1)} %refs_2_.1, s32[3,4,512]{2,1,0:T(4,128)} %refs_3_.1, s32[3,4,512]{2,1,0:T(4,128)} %refs_4_.1, bf16[256,512]{1,0:T(8,128)(2,1)} %constant.4.clone.refs_5_.table_ref), custom_call_target="tpu_custom_call" | custom-call | tf_op jit(solution)/shard_map/spectra/pallas_call | solution.py:84
  7.7 170.6 %all_to_all.22 = bf16[128,8,1536]{2,1,0:T(8,128)(2,1)S(1)} all-to-all(bf16[128,8,1536]{2,1,0:T(8,128)(2,1)S(1)} %bitcast.5), channel_id=1, replica_groups=mesh['groups'=2,'freq'=128] {'freq'}, dimensions={0} | all-to-all | bytes 6291456 | tf_op jit(solution)/shard_map/all_to_all | solution.py:181
  178.3 3.8 %product.1 = bf16[1024,512]{1,0:T(8,128)(2,1)S(1)} custom-call(bf16[1024,1536]{1,0:T(8,128)(2,1)S(1)} %bitcast.4, bf16[256,256]{1,0:T(8,128)(2,1)} %constant.5.clone.swap_ref), custom_call_target="tpu_custom_call" | custom-call | tf_op jit(solution)/shard_map/product/pallas_call | solution.py:127
  182.1 63.7 %all_to_all.23 = bf16[128,8,512]{2,1,0:T(8,128)(2,1)S(1)} all-to-all(bf16[128,8,512]{2,1,0:T(8,128)(2,1)S(1)} %bitcast.7), channel_id=1, replica_groups=mesh['groups'=2,'freq'=128] {'freq'}, dimensions={0} | all-to-all | bytes 2097152 | tf_op jit(solution)/shard_map/all_to_all | solution.py:184
  245.8 2.7 %inverse.1 = bf16[4,512,512]{2,1,0:T(8,128)(2,1)} custom-call(bf16[1024,512]{1,0:T(8,128)(2,1)S(1)} %bitcast.6, bf16[256,512]{1,0:T(8,128)(2,1)} %constant.4.clone.refs_5_.table_ref), custom_call_target="tpu_custom_call" | custom-call | tf_op jit(solution)/shard_map/inverse/pallas_call | solution.py:160
